TPU v7x, 128 devices: a whole 4x4x4 slice. The times are simulated.
128 devices in a mesh: section: 8 (over x, core), expert: 4 (over y), dp: 4 (over z).
Axes of the slice: x: 4, y: 4, z: 4, core: 2. Of those that a mesh axis runs over, the one named last changes fastest.
Arguments:
- x_in: bfloat16 [8, 256, 2048], P(None, ('expert', 'dp'), 'section'), may hold values from -6 to 6
- cotangent: bfloat16 [8, 256, 2048], P(None, ('expert', 'dp'), 'section'), may hold values from -6 to 6
- route_ids: int32 [8, 8, 256, 2], P('section', None, ('expert', 'dp')), may hold values from 0 to 15, all different within a row; in each aligned block of 16 rows (0 to 15, 16 to 31, ..., all dimensions but the last counted through in order) at most 2 rows name the same one
- norm_gain: float32 [8, 2048], P('section'), may hold values from 0.5 to 1.5
- router: bfloat16 [8, 2048, 16], P('section'), may hold values from -0.125 to 0.125
- w_gate_up: bfloat16 [8, 16, 2048, 1024], P('section', ('expert', 'dp')), may hold values from -0.125 to 0.125
- w_down: bfloat16 [8, 16, 512, 2048], P('section', ('expert', 'dp')), may hold values from -0.25 to 0.25
Outputs:
- grad_in: bfloat16 [8, 256, 2048], P(None, ('expert', 'dp'), 'section')
- grad_gate_up: float32 [8, 16, 2048, 1024], P('section', ('expert', 'dp'))
- grad_down: float32 [8, 16, 512, 2048], P('section', ('expert', 'dp'))
- grad_router: float32 [8, 2048, 16], P('section')
- grad_gain: float32 [8, 2048], P('section')
Inputs may be any that keep to these rules, and one draw needn't show every extreme that they name: `route_ids`: each row names two different experts; the 16 rows of one device in one layer and micro-batch name any expert at most 2 times, a bound that some block reaches in some of them.
All inputs are finite; a program needn't handle non-finite values.
Results may differ from a plain program's by a relative error of at most 0.035.
Values may be sent and summed in bfloat16 or wider, within the bound.
No kernel may reach another device: no remote copies, remote signals or barrier semaphores. Data moves between devices by JAX's collectives and lax.ppermute only.
A program may use at most 64 MiB of HBM per device.

v0:
```python
import jax
import jax.numpy as jnp
from jax import lax
from jax.sharding import PartitionSpec as P

EPS = 1e-05


def sent_together(arrays, axis, dim, along):
    widths = [a.shape[along] for a in arrays]
    both = jnp.concatenate(arrays, axis=along)
    whole = lax.all_gather(both, axis, axis=dim, tiled=True)
    return tuple(jnp.split(whole, [sum(widths[:k]) for k in range(1, len(widths))], axis=along))


def shifted(value, axis, steps):
    count = lax.axis_size(axis)
    leading, last = (max(0, -steps), min(count, count - steps))
    return lax.ppermute(value, axis, [(source, source + steps) for source in range(leading, last)])


def copy_for_each(shard, axis):
    copies = jnp.broadcast_to(shard, (lax.axis_size(axis), *shard.shape))
    return lax.all_to_all(copies, axis, split_axis=0, concat_axis=0, tiled=True)


def of_everyone(shard, axis):
    return copy_for_each(shard, axis).astype(jnp.float32).sum(axis=0)


def in_blocks(shard, dim, length):
    before, after = (shard.shape[:dim], shard.shape[dim + 1 :])
    return jnp.moveaxis(shard.reshape(*before, length, -1, *after), dim, 0)


def sent_and_summed(shard, axis, dim):
    length = lax.axis_size(axis)
    pieces = lax.all_to_all(in_blocks(shard, dim, length), axis, 0, 0, tiled=True)
    return jnp.sum(pieces.astype(jnp.float32), axis=0)


def keep_row(stash, position, value, active):
    old_row = lax.dynamic_index_in_dim(stash, position, 0, keepdims=False)
    return lax.dynamic_update_index_in_dim(stash, jnp.where(active, value, old_row), position, 0)


def slot_tables(route_rows, n_expert, capacity):
    experts = jnp.arange(n_expert, dtype=jnp.int32)
    expert_hits = (route_rows[:, :, None] == experts).astype(jnp.int32)
    per_expert = jnp.sum(expert_hits, axis=1)
    before = jnp.cumsum(per_expert, axis=0) - per_expert
    slot_ids = jnp.sum(expert_hits * before[:, None, :], axis=2)
    dest_cell = jnp.transpose(route_rows * capacity + slot_ids)
    cell_ids = jnp.arange(n_expert * capacity, dtype=jnp.int32)
    slot_place = (dest_cell[:, :, None] == cell_ids).astype(jnp.bfloat16)
    return (expert_hits.astype(jnp.float32), slot_place)


def norm_rows(layer_in, gain_vec):
    h_wide = layer_in.astype(jnp.float32)
    inv_rms = lax.rsqrt(jnp.mean(h_wide * h_wide, axis=-1, keepdims=True) + EPS)
    normed = (h_wide * inv_rms * gain_vec).astype(jnp.bfloat16)
    return (h_wide, inv_rms, normed)


def pair_gates(normed, router_mat, expert_hits):
    logits = jnp.dot(normed, router_mat, preferred_element_type=jnp.float32)
    chosen = jnp.sum(expert_hits * logits[:, None, :], axis=2)
    return (
        jax.nn.sigmoid(chosen[:, 0] - chosen[:, 1]),
        jax.nn.sigmoid(chosen[:, 1] - chosen[:, 0]),
    )


def expert_inner(exp_rows, w_gu):
    gate_up = jnp.einsum("sekd,edf->sekf", exp_rows, w_gu, preferred_element_type=jnp.float32)
    half_cols = w_gu.shape[2] // 2
    gate_part = gate_up[..., :half_cols]
    up_part = gate_up[..., half_cols:]
    sigmoid_gate = jax.nn.sigmoid(gate_part)
    hidden = (gate_part * sigmoid_gate * up_part).astype(jnp.bfloat16)
    return (gate_part, up_part, sigmoid_gate, hidden)


def expert_grads(gate_part, up_part, sigmoid_gate, dy_rows, w_gu, w_dn):
    d_hidden = jnp.einsum("sekd,efd->sekf", dy_rows, w_dn, preferred_element_type=jnp.float32)
    silu_gate = gate_part * sigmoid_gate
    silu_slope = sigmoid_gate * (1.0 + gate_part * (1.0 - sigmoid_gate))
    gate_up_grad = jnp.concatenate(
        [d_hidden * up_part * silu_slope, d_hidden * silu_gate], axis=-1
    ).astype(jnp.bfloat16)
    rows_grad = jnp.einsum(
        "sekf,edf->sekd", gate_up_grad, w_gu, preferred_element_type=jnp.float32
    ).astype(jnp.bfloat16)
    return (gate_up_grad, rows_grad)


def local(x_in, cotangent, route_ids, norm_gain, router, w_gate_up, w_down):
    micro_count, tok_rows, _ = x_in.shape
    n_segment = lax.axis_size("section")
    n_rank = lax.axis_size("expert") * lax.axis_size("dp")
    per_rank = w_down.shape[1]
    hidden_width = w_down.shape[2]
    model_width = w_down.shape[3]
    n_expert = per_rank * n_rank
    capacity = tok_rows * 2 * 9 // (8 * n_expert)
    cells = n_expert * capacity
    segment_idx = lax.axis_index("section")
    rows_shape = (n_rank, per_rank, capacity, model_width)
    x_all, top_all = sent_together((x_in, cotangent), "section", 2, 0)
    route_all = route_ids[0]
    gain_vec = norm_gain[0]
    router_mat = router[0]
    router_wide = router_mat.astype(jnp.float32)
    w_gu = w_gate_up[0]
    w_dn = w_down[0]
    ticks = micro_count + n_segment - 1

    def expert_forward(piece_rows):
        _, _, _, hidden = expert_inner(piece_rows, w_gu)
        out_rows = jnp.einsum(
            "sekf,efd->sekd", hidden, w_dn, preferred_element_type=jnp.float32
        ).astype(jnp.bfloat16)
        return (
            lax.all_to_all(out_rows, ("expert", "dp"), split_axis=0, concat_axis=0, tiled=True),
            piece_rows,
        )

    def forward_tick(tick_no, state_in):
        received, stash_h, stash_y, stash_x = state_in
        tick_slot = tick_no - segment_idx
        active = (tick_slot >= 0) & (tick_slot < micro_count)
        micro_idx = jnp.clip(tick_slot, 0, micro_count - 1)
        fresh_in = lax.dynamic_index_in_dim(x_all, micro_idx, 0, keepdims=False)
        layer_in = jnp.where(segment_idx == 0, fresh_in, received)
        h_wide, inv_rms, normed = norm_rows(layer_in, gain_vec)
        route_rows = lax.dynamic_index_in_dim(route_all, micro_idx, 0, keepdims=False)
        expert_hits, slot_place = slot_tables(route_rows, n_expert, capacity)
        send_rows = jnp.einsum("ktc,td->cd", slot_place, normed, preferred_element_type=jnp.float32)
        send_rows = send_rows.astype(jnp.bfloat16).reshape(rows_shape)
        returned, landed = expert_forward(
            lax.all_to_all(send_rows, ("expert", "dp"), split_axis=0, concat_axis=0, tiled=True)
        )
        back_flat = returned.reshape(cells, model_width)
        picked = jnp.einsum(
            "ktc,cd->ktd", slot_place, back_flat, preferred_element_type=jnp.float32
        )
        first_gate, second_gate = pair_gates(normed, router_mat, expert_hits)
        layer_out = (
            h_wide + first_gate[:, None] * picked[0] + second_gate[:, None] * picked[1]
        ).astype(jnp.bfloat16)
        passed = shifted(layer_out, "section", 1)
        stash_h = keep_row(stash_h, micro_idx, layer_in, active)
        stash_y = keep_row(stash_y, micro_idx, back_flat, active)
        stash_x = keep_row(stash_x, micro_idx, landed, active)
        return (passed, stash_h, stash_y, stash_x)

    start_fwd = (
        jnp.zeros((tok_rows, model_width), jnp.bfloat16),
        jnp.zeros((micro_count, tok_rows, model_width), jnp.bfloat16),
        jnp.zeros((micro_count, cells, model_width), jnp.bfloat16),
        jnp.zeros((micro_count,) + rows_shape, jnp.bfloat16),
    )
    _, stash_h, stash_y, stash_x = lax.fori_loop(0, ticks, forward_tick, start_fwd)

    def backward_tick(tick_no, state_in):
        received, keep_rows, keep_dy, keep_hidden, keep_dab, stash_grad, acc_router, acc_gain = (
            state_in
        )
        tick_slot = tick_no - (n_segment - 1 - segment_idx)
        active = (tick_slot >= 0) & (tick_slot < micro_count)
        micro_idx = jnp.clip(tick_slot, 0, micro_count - 1)
        fresh_top = lax.dynamic_index_in_dim(top_all, micro_idx, 0, keepdims=False)
        grad_top = jnp.where(segment_idx == n_segment - 1, fresh_top, received)
        grad_wide = grad_top.astype(jnp.float32)
        layer_in = lax.dynamic_index_in_dim(stash_h, micro_idx, 0, keepdims=False)
        h_wide, inv_rms, normed = norm_rows(layer_in, gain_vec)
        route_rows = lax.dynamic_index_in_dim(route_all, micro_idx, 0, keepdims=False)
        expert_hits, slot_place = slot_tables(route_rows, n_expert, capacity)
        first_gate, second_gate = pair_gates(normed, router_mat, expert_hits)
        gates = jnp.stack([first_gate, second_gate])
        scaled = (gates[:, :, None] * grad_wide[None]).astype(jnp.bfloat16)
        dy_send = jnp.einsum("ktc,ktd->cd", slot_place, scaled, preferred_element_type=jnp.float32)
        dy_send = dy_send.astype(jnp.bfloat16).reshape(rows_shape)
        exp_rows = lax.dynamic_index_in_dim(stash_x, micro_idx, 0, keepdims=False)
        dy_rows = lax.all_to_all(dy_send, ("expert", "dp"), split_axis=0, concat_axis=0, tiled=True)
        gate_part, up_part, sigmoid_gate, hidden = expert_inner(exp_rows, w_gu)
        gate_up_grad, rows_grad = expert_grads(
            gate_part, up_part, sigmoid_gate, dy_rows, w_gu, w_dn
        )
        back_grad = lax.all_to_all(
            rows_grad, ("expert", "dp"), split_axis=0, concat_axis=0, tiled=True
        )
        back_y = lax.dynamic_index_in_dim(stash_y, micro_idx, 0, keepdims=False)
        keep_dy = keep_row(keep_dy, micro_idx, dy_rows, active)
        keep_hidden = keep_row(keep_hidden, micro_idx, hidden, active)
        keep_dab = keep_row(keep_dab, micro_idx, gate_up_grad, active)
        normed_grad = jnp.einsum(
            "ktc,cd->td",
            slot_place,
            back_grad.reshape(cells, model_width),
            preferred_element_type=jnp.float32,
        )
        picked = jnp.einsum("ktc,cd->ktd", slot_place, back_y, preferred_element_type=jnp.float32)
        gate_grad = jnp.sum(grad_wide[None] * picked, axis=-1)
        logit_grad = first_gate * second_gate * (gate_grad[0] - gate_grad[1])
        logit_cols = logit_grad[:, None] * (expert_hits[:, 0, :] - expert_hits[:, 1, :])
        normed_grad = normed_grad + jnp.dot(logit_cols, router_wide.T)
        router_term = jnp.dot(normed.astype(jnp.float32).T, logit_cols)
        acc_router = acc_router + jnp.where(active, router_term, 0.0)
        acc_gain = acc_gain + jnp.where(
            active, jnp.sum(normed_grad * h_wide * inv_rms, axis=0), 0.0
        )
        scaled_grad = normed_grad * gain_vec
        projection = jnp.mean(scaled_grad * h_wide, axis=-1, keepdims=True)
        input_grad = (
            grad_wide + inv_rms * scaled_grad - h_wide * inv_rms * inv_rms * inv_rms * projection
        )
        grad_sent = input_grad.astype(jnp.bfloat16)
        stash_grad = keep_row(stash_grad, micro_idx, grad_sent, active)
        passed = shifted(grad_sent, "section", -1)
        return (passed, keep_rows, keep_dy, keep_hidden, keep_dab, stash_grad, acc_router, acc_gain)

    start_bwd = (
        jnp.zeros((tok_rows, model_width), jnp.bfloat16),
        stash_x,
        jnp.zeros((micro_count,) + rows_shape, jnp.bfloat16),
        jnp.zeros((micro_count, n_rank, per_rank, capacity, hidden_width), jnp.bfloat16),
        jnp.zeros((micro_count, n_rank, per_rank, capacity, 2 * hidden_width), jnp.bfloat16),
        jnp.zeros((micro_count, tok_rows, model_width), jnp.bfloat16),
        jnp.zeros((model_width, n_expert), jnp.float32),
        jnp.zeros((model_width,), jnp.float32),
    )
    final = lax.fori_loop(0, ticks, backward_tick, start_bwd)
    _, keep_rows, keep_dy, keep_hidden, keep_dab, stash_grad, acc_router, acc_gain = final
    grad_gu = jnp.einsum(
        "msekd,msekf->edf", keep_rows, keep_dab, preferred_element_type=jnp.float32
    )
    grad_dn = jnp.einsum(
        "msekf,msekd->efd", keep_hidden, keep_dy, preferred_element_type=jnp.float32
    )
    sum_router, sum_gain = (
        of_everyone(acc_router.astype(jnp.bfloat16), ("expert", "dp")).astype(jnp.float32),
        of_everyone(acc_gain.astype(jnp.bfloat16), ("expert", "dp")).astype(jnp.float32),
    )
    first_term = jnp.where(segment_idx == 0, stash_grad.astype(jnp.float32), 0.0)
    grad_in = sent_and_summed(first_term.astype(jnp.bfloat16), "section", 2).astype(jnp.bfloat16)
    return (grad_in, grad_gu[None], grad_dn[None], sum_router[None], sum_gain[None])


def solution(mesh):
    in_specs = (
        P(None, ("expert", "dp"), "section"),
        P(None, ("expert", "dp"), "section"),
        P("section", None, ("expert", "dp"), None),
        P("section", None),
        P("section", None, None),
        P("section", ("expert", "dp"), None, None),
        P("section", ("expert", "dp"), None, None),
    )
    out_specs = (
        P(None, ("expert", "dp"), "section"),
        P("section", ("expert", "dp"), None, None),
        P("section", ("expert", "dp"), None, None),
        P("section", None, None),
        P("section", None),
    )
    return jax.shard_map(local, mesh=mesh, in_specs=in_specs, out_specs=out_specs, check_vma=False)
```

profile of v0, /device:TPU:0, one launch (start us, length us, event | category | flops | bytes accessed | tf_op | source)
XLA Modules:
  0.0 1300.0 jit_solution(4501914240552446879)
XLA Ops:
  9.0 27.0 %all-gather.2.cloned.1.call-done = bf16[16,16,2048]{2,1,0:T(8,128)(2,1)} async-done(((bf16[16,16,256]{2,1,0:T(8,128)(2,1)}), bf16[16,16,2048]{2,1,0:T(8,128)(2,1)}) %all-gather.2.cloned.1.call-update) | async-done | bytes 1048592 | tf_op jit(solution)/shard_map/all_gather | solution.py:12
  41.2 551.5 %while.48 = (s32[]{:T(128)}, bf16[16,2048]{1,0:T(8,128)(2,1)S(1)}, bf16[8,16,2048]{2,1,0:T(8,128)(2,1)S(1)}, bf16[8,32,2048]{2,1,0:T(8,128)(2,1)}, bf16[8,16,1,2...) while((s32[]{:T(128)}, bf16[16,2048]{1,0:T(8,128)(2,1)S(1)}, ...), condition=%wide.region_7.8_spmd, body=%wide.region_0.7_spmd.sunk | while | flops 209598352 | bytes 11630114 | solution.py:164
  68.5 7.1 all-to-all-done.1
  103.0 7.2 all-to-all-done.1
  173.7 7.0 all-to-all-done.1
  247.5 7.1 all-to-all-done.1
  284.4 7.0 all-to-all-done.1
  596.8 642.6 %while.49 = (s32[]{:T(128)}, bf16[16,2048]{1,0:T(8,128)(2,1)S(1)}, bf16[8,16,1,2,2048]{4,3,1,2,0:T(2,128)(2,1)}, bf16[8,16,1,2,512]{4,1,3,2,0:T(8,128)(2,1)}, bf...) while((s32[]{:T(128)}, bf16[16,2048]{1,0:T(8,128)(2,1)S(1)}, ...), condition=%wide.region_18.19_spmd.clone, body=%wide.region_8.18_spmd.clone.sunk | while | flops 351425984 | bytes 17749480 | solution.py:234
  618.8 7.2 all-to-all-start.3
  662.4 7.2 all-to-all-start.3
  706.6 7.1 all-to-all-start.3
  749.0 7.1 all-to-all-start.3
  791.7 7.1 all-to-all-start.3
  834.4 7.1 all-to-all-start.3
  877.1 7.1 all-to-all-start.3
  919.8 7.1 all-to-all-start.3
  962.5 7.1 all-to-all-start.3
  1005.2 7.1 all-to-all-start.3
  1047.9 7.1 all-to-all-start.3
  1090.6 7.1 all-to-all-start.3
  1133.3 7.1 all-to-all-start.3
  1176.0 7.1 all-to-all-start.3
  1218.7 7.1 all-to-all-start.3
  1280.1 12.3 all-to-all-done.5
  (1379 shorter events, 1100.3 us)
Async XLA Ops:
  7.2 28.8 %all-gather.2.cloned.1.call-start = ((), (), s32[]{:S(2)}) async-start(), calls=%async_computation.7 | async-start | bytes 1179648 | tf_op jit(solution)/shard_map/all_gather | solution.py:12
  45.0 14.8 %all-to-all-start = ((bf16[16,1,2,2048]{3,2,1,0:T(2,128)(2,1)}), bf16[16,1,2,2048]{3,2,1,0:T(2,128)(2,1)S(1)}, u32[]{:S(2)}, u32[]{:S(2)}) async-start(bf16[16,1,2,2048]{3,2,1,0:T(2,128)(2,1)} %bitcast.333), calls=%async_computation | async-start | bytes 262144 | tf_op jit(solution)/shard_map/while/body/eval_jaxpr/all_to_all | solution.py:142
  82.7 11.5 all-to-all-start
  98.4 11.7 all-to-all-start.1
  618.8 15.0 %all-to-all-start.3 = ((bf16[16,1,2,2048]{3,2,1,0:T(2,128)(2,1)}), bf16[16,1,2,2048]{3,2,1,0:T(2,128)(2,1)S(1)}, u32[]{:S(2)}, u32[]{:S(2)}) async-start(bf16[16,1,2,2048]{3,2,1,0:T(2,128)(2,1)} %copy.132), calls=%async_computation.3 | async-start | bytes 262144 | tf_op jit(solution)/shard_map/while/body/eval_jaxpr/all_to_all | solution.py:191
  662.4 15.0 %all-to-all-start.3 = ((bf16[16,1,2,2048]{3,2,1,0:T(2,128)(2,1)}), bf16[16,1,2,2048]{3,2,1,0:T(2,128)(2,1)S(1)}, u32[]{:S(2)}, u32[]{:S(2)}) async-start(bf16[16,1,2,2048]{3,2,1,0:T(2,128)(2,1)} %copy.132), calls=%async_computation.3 | async-start | bytes 262144 | tf_op jit(solution)/shard_map/while/body/eval_jaxpr/all_to_all | solution.py:191
  690.0 11.5 all-to-all-start.2
  706.6 14.9 %all-to-all-start.3 = ((bf16[16,1,2,2048]{3,2,1,0:T(2,128)(2,1)}), bf16[16,1,2,2048]{3,2,1,0:T(2,128)(2,1)S(1)}, u32[]{:S(2)}, u32[]{:S(2)}) async-start(bf16[16,1,2,2048]{3,2,1,0:T(2,128)(2,1)} %copy.132), calls=%async_computation.3 | async-start | bytes 262144 | tf_op jit(solution)/shard_map/while/body/eval_jaxpr/all_to_all | solution.py:191
  732.4 11.5 all-to-all-start.2
  749.0 14.9 %all-to-all-start.3 = ((bf16[16,1,2,2048]{3,2,1,0:T(2,128)(2,1)}), bf16[16,1,2,2048]{3,2,1,0:T(2,128)(2,1)S(1)}, u32[]{:S(2)}, u32[]{:S(2)}) async-start(bf16[16,1,2,2048]{3,2,1,0:T(2,128)(2,1)} %copy.132), calls=%async_computation.3 | async-start | bytes 262144 | tf_op jit(solution)/shard_map/while/body/eval_jaxpr/all_to_all | solution.py:191
  791.7 14.9 %all-to-all-start.3 = ((bf16[16,1,2,2048]{3,2,1,0:T(2,128)(2,1)}), bf16[16,1,2,2048]{3,2,1,0:T(2,128)(2,1)S(1)}, u32[]{:S(2)}, u32[]{:S(2)}) async-start(bf16[16,1,2,2048]{3,2,1,0:T(2,128)(2,1)} %copy.132), calls=%async_computation.3 | async-start | bytes 262144 | tf_op jit(solution)/shard_map/while/body/eval_jaxpr/all_to_all | solution.py:191
  834.4 14.9 %all-to-all-start.3 = ((bf16[16,1,2,2048]{3,2,1,0:T(2,128)(2,1)}), bf16[16,1,2,2048]{3,2,1,0:T(2,128)(2,1)S(1)}, u32[]{:S(2)}, u32[]{:S(2)}) async-start(bf16[16,1,2,2048]{3,2,1,0:T(2,128)(2,1)} %copy.132), calls=%async_computation.3 | async-start | bytes 262144 | tf_op jit(solution)/shard_map/while/body/eval_jaxpr/all_to_all | solution.py:191
  860.5 11.5 all-to-all-start.2
  877.1 14.9 %all-to-all-start.3 = ((bf16[16,1,2,2048]{3,2,1,0:T(2,128)(2,1)}), bf16[16,1,2,2048]{3,2,1,0:T(2,128)(2,1)S(1)}, u32[]{:S(2)}, u32[]{:S(2)}) async-start(bf16[16,1,2,2048]{3,2,1,0:T(2,128)(2,1)} %copy.132), calls=%async_computation.3 | async-start | bytes 262144 | tf_op jit(solution)/shard_map/while/body/eval_jaxpr/all_to_all | solution.py:191
  919.8 14.9 %all-to-all-start.3 = ((bf16[16,1,2,2048]{3,2,1,0:T(2,128)(2,1)}), bf16[16,1,2,2048]{3,2,1,0:T(2,128)(2,1)S(1)}, u32[]{:S(2)}, u32[]{:S(2)}) async-start(bf16[16,1,2,2048]{3,2,1,0:T(2,128)(2,1)} %copy.132), calls=%async_computation.3 | async-start | bytes 262144 | tf_op jit(solution)/shard_map/while/body/eval_jaxpr/all_to_all | solution.py:191
  962.5 14.9 %all-to-all-start.3 = ((bf16[16,1,2,2048]{3,2,1,0:T(2,128)(2,1)}), bf16[16,1,2,2048]{3,2,1,0:T(2,128)(2,1)S(1)}, u32[]{:S(2)}, u32[]{:S(2)}) async-start(bf16[16,1,2,2048]{3,2,1,0:T(2,128)(2,1)} %copy.132), calls=%async_computation.3 | async-start | bytes 262144 | tf_op jit(solution)/shard_map/while/body/eval_jaxpr/all_to_all | solution.py:191
  1005.2 15.0 %all-to-all-start.3 = ((bf16[16,1,2,2048]{3,2,1,0:T(2,128)(2,1)}), bf16[16,1,2,2048]{3,2,1,0:T(2,128)(2,1)S(1)}, u32[]{:S(2)}, u32[]{:S(2)}) async-start(bf16[16,1,2,2048]{3,2,1,0:T(2,128)(2,1)} %copy.132), calls=%async_computation.3 | async-start | bytes 262144 | tf_op jit(solution)/shard_map/while/body/eval_jaxpr/all_to_all | solution.py:191
  1047.9 14.9 %all-to-all-start.3 = ((bf16[16,1,2,2048]{3,2,1,0:T(2,128)(2,1)}), bf16[16,1,2,2048]{3,2,1,0:T(2,128)(2,1)S(1)}, u32[]{:S(2)}, u32[]{:S(2)}) async-start(bf16[16,1,2,2048]{3,2,1,0:T(2,128)(2,1)} %copy.132), calls=%async_computation.3 | async-start | bytes 262144 | tf_op jit(solution)/shard_map/while/body/eval_jaxpr/all_to_all | solution.py:191
  1090.6 14.9 %all-to-all-start.3 = ((bf16[16,1,2,2048]{3,2,1,0:T(2,128)(2,1)}), bf16[16,1,2,2048]{3,2,1,0:T(2,128)(2,1)S(1)}, u32[]{:S(2)}, u32[]{:S(2)}) async-start(bf16[16,1,2,2048]{3,2,1,0:T(2,128)(2,1)} %copy.132), calls=%async_computation.3 | async-start | bytes 262144 | tf_op jit(solution)/shard_map/while/body/eval_jaxpr/all_to_all | solution.py:191
  1133.3 14.9 %all-to-all-start.3 = ((bf16[16,1,2,2048]{3,2,1,0:T(2,128)(2,1)}), bf16[16,1,2,2048]{3,2,1,0:T(2,128)(2,1)S(1)}, u32[]{:S(2)}, u32[]{:S(2)}) async-start(bf16[16,1,2,2048]{3,2,1,0:T(2,128)(2,1)} %copy.132), calls=%async_computation.3 | async-start | bytes 262144 | tf_op jit(solution)/shard_map/while/body/eval_jaxpr/all_to_all | solution.py:191
  1176.0 15.0 %all-to-all-start.3 = ((bf16[16,1,2,2048]{3,2,1,0:T(2,128)(2,1)}), bf16[16,1,2,2048]{3,2,1,0:T(2,128)(2,1)S(1)}, u32[]{:S(2)}, u32[]{:S(2)}) async-start(bf16[16,1,2,2048]{3,2,1,0:T(2,128)(2,1)} %copy.132), calls=%async_computation.3 | async-start | bytes 262144 | tf_op jit(solution)/shard_map/while/body/eval_jaxpr/all_to_all | solution.py:191
  1218.7 14.9 %all-to-all-start.3 = ((bf16[16,1,2,2048]{3,2,1,0:T(2,128)(2,1)}), bf16[16,1,2,2048]{3,2,1,0:T(2,128)(2,1)S(1)}, u32[]{:S(2)}, u32[]{:S(2)}) async-start(bf16[16,1,2,2048]{3,2,1,0:T(2,128)(2,1)} %copy.132), calls=%async_computation.3 | async-start | bytes 262144 | tf_op jit(solution)/shard_map/while/body/eval_jaxpr/all_to_all | solution.py:191
  1253.0 17.0 %all-to-all-start.4 = ((bf16[8,8,16,256]{3,2,1,0:T(8,128)(2,1)}), bf16[8,8,16,256]{3,2,1,0:T(8,128)(2,1)S(1)}, u32[]{:S(2)}, u32[]{:S(2)}) async-start(bf16[8,8,16,256]{3,2,1,0:T(8,128)(2,1)} %copy.92), calls=%async_computation.4 | async-start | bytes 1048576 | tf_op jit(solution)/shard_map/all_to_all | solution.py:38
  1271.0 21.3 %all-to-all-start.5 = ((bf16[16,2048,16]{1,2,0:T(8,128)(2,1)}), bf16[16,2048,16]{1,2,0:T(8,128)(2,1)S(1)}, u32[]{:S(2)}, u32[]{:S(2)}) async-start(bf16[16,2048,16]{1,2,0:T(8,128)(2,1)} %broadcast_in_dim.180), calls=%async_computation.5 | async-start | bytes 2097152 | tf_op jit(solution)/shard_map/all_to_all | solution.py:24
  (196 other events, 2629.8 us)
Sparse Core Ops, SparseCore 0:
  10.3 25.7 all-gather.1
where the time goes:
time: 1310 us; the launch traced here: 1300 us
  waiting for transfers between devices  387 us (30%)
  starting transfers between devices  358 us (27%)
  matrix products  217 us (17%)
  other arithmetic  167 us (13%)
  local copies, waits for them, and re-layouts  152 us (12%)
  between operations  14.2 us (1%)
    all_to_all x15, starting transfers between devices, backward_tick(): lax.all_to_all(rows_grad, ('expert', 'dp'), split_axis=0, concat_axis=0,...  107 us
    all_to_all x15, waiting for transfers between devices, expert_forward(): lax.all_to_all(out_rows, ('expert', 'dp'), split_axis=0, concat_axis=0, t...  106 us
    dynamic_update_slice x105, other arithmetic, keep_row(): lax.dynamic_update_index_in_dim(stash, jnp.where(active, value, old_row),...  104 us
    all_to_all x15, waiting for transfers between devices, forward_tick(): lax.all_to_all(send_rows, ('expert', 'dp'), split_axis=0, concat_axis=0,...  96.6 us
    dot_general x30, matrix products, expert_inner(): jnp.einsum('sekd,edf->sekf', exp_rows, w_gu, preferred_element_type=jnp.f...  90.3 us
    all_to_all x15, waiting for transfers between devices, backward_tick(): lax.all_to_all(rows_grad, ('expert', 'dp'), split_axis=0, concat_axis=0,...  83.5 us
    ppermute x30, starting transfers between devices, shifted(): lax.ppermute(value, axis, [(source, source + steps) for source in range(l...  71.8 us
    all_to_all x15, starting transfers between devices, forward_tick(): lax.all_to_all(send_rows, ('expert', 'dp'), split_axis=0, concat_axis=0,...  57.7 us
  transfers between devices with their start and end apart: 94, of which 79 were waited for; matrix products, arithmetic and copies ran while one was open for 17% of the time, Pallas kernels for 0%

commit v1 on v0

v1 whole, which is shorter than its diff:
```python
import jax
import jax.numpy as jnp
from jax import lax
from jax.sharding import PartitionSpec as P

EPS = 1e-05
ED = ("expert", "dp")


def swapped(value):
    count = lax.axis_size("section")
    return lax.ppermute(value, "section", [(s, s ^ 1) for s in range(count)])


def rotated(value, steps):
    count = lax.axis_size("section")
    return lax.ppermute(value, "section", [(s, (s + steps) % count) for s in range(count)])


def exchanged(rows, axis):
    return lax.all_to_all(rows, axis, split_axis=0, concat_axis=0, tiled=True)


def chosen(first, mine, other):
    return (jnp.where(first, mine, other), jnp.where(first, other, mine))


def route_tables(route_rows, n_expert, capacity):
    micro_count, tok_rows, _ = route_rows.shape
    experts = jnp.arange(n_expert, dtype=jnp.int32)
    hits = (route_rows[..., None] == experts).astype(jnp.int32)
    per_expert = jnp.sum(hits, axis=2)
    before = jnp.cumsum(per_expert, axis=1) - per_expert
    slot_ids = jnp.sum(hits * before[:, :, None, :], axis=3)
    micro_ids = jnp.arange(micro_count, dtype=jnp.int32)[:, None, None]
    cell = (route_rows * micro_count + micro_ids) * capacity + slot_ids
    cell = jnp.transpose(cell, (2, 0, 1)).reshape(2 * micro_count * tok_rows)
    cell_ids = jnp.arange(n_expert * micro_count * capacity, dtype=jnp.int32)
    place = (cell[:, None] == cell_ids).astype(jnp.bfloat16)
    diff = (hits[:, :, 0, :] - hits[:, :, 1, :]).astype(jnp.float32)
    return place, diff.reshape(micro_count * tok_rows, n_expert)


def dot(a, b, dims):
    return lax.dot_general(a, b, (dims, ((), ())), preferred_element_type=jnp.float32)


def forward_layer(h, wt, n_rank):
    place, diff, gain, router, w_gu, w_dn = wt
    tokens, width = h.shape
    both = place[:tokens] + place[tokens:]
    h_wide = h.astype(jnp.float32)
    inv = lax.rsqrt(jnp.mean(h_wide * h_wide, axis=-1, keepdims=True) + EPS)
    u = (h_wide * inv * gain).astype(jnp.bfloat16)
    send = dot(both, u, ((0,), (0,))).astype(jnp.bfloat16)
    rows = exchanged(send.reshape(n_rank, -1, width), ED).reshape(-1, width)
    logits = dot(u, router, ((1,), (0,)))
    delta = jnp.sum(diff * logits, axis=1, keepdims=True)
    g1, g2 = jax.nn.sigmoid(delta), jax.nn.sigmoid(-delta)
    gate_up = dot(rows, w_gu, ((1,), (0,)))
    half = w_gu.shape[1] // 2
    a, b = gate_up[:, :half], gate_up[:, half:]
    sig = jax.nn.sigmoid(a)
    hidden = (a * sig * b).astype(jnp.bfloat16)
    out = dot(hidden, w_dn, ((1,), (0,))).astype(jnp.bfloat16)
    back = exchanged(out.reshape(n_rank, -1, width), ED).reshape(-1, width)
    y = dot(place, back, ((1,), (0,)))
    y1, y2 = y[:tokens], y[tokens:]
    h_next = (h_wide + g1 * y1 + g2 * y2).astype(jnp.bfloat16)
    saved = (h, inv, u, g1, g2, rows, gate_up, hidden, y.astype(jnp.bfloat16))
    return h_next, saved


def backward_layer(grad, wt, saved, n_rank):
    place, diff, gain, router, w_gu, w_dn = wt
    h, inv, u, g1, g2, rows, gate_up, hidden, y = saved
    tokens, width = h.shape
    both = place[:tokens] + place[tokens:]
    half = w_gu.shape[1] // 2
    h_wide = h.astype(jnp.float32)
    g_wide = grad.astype(jnp.float32)
    scaled = jnp.concatenate([(g1 * g_wide).astype(jnp.bfloat16), (g2 * g_wide).astype(jnp.bfloat16)], axis=0)
    dy_send = dot(place, scaled, ((0,), (0,))).astype(jnp.bfloat16)
    dy = exchanged(dy_send.reshape(n_rank, -1, width), ED).reshape(-1, width)
    c1 = jnp.sum(g_wide * y[:tokens].astype(jnp.float32), axis=-1, keepdims=True)
    c2 = jnp.sum(g_wide * y[tokens:].astype(jnp.float32), axis=-1, keepdims=True)
    logit_cols = g1 * g2 * (c1 - c2) * diff
    through_router = dot(logit_cols, router.astype(jnp.float32), ((1,), (1,)))
    router_part = dot(logit_cols, u.astype(jnp.float32), ((0,), (0,)))
    a, b = gate_up[:, :half], gate_up[:, half:]
    sig = jax.nn.sigmoid(a)
    d_hidden = dot(dy, w_dn, ((1,), (1,)))
    q = jnp.concatenate(
        [d_hidden * b * (sig * (1.0 + a * (1.0 - sig))), d_hidden * (a * sig)], axis=-1
    ).astype(jnp.bfloat16)
    du_rows = dot(q, w_gu, ((1,), (1,))).astype(jnp.bfloat16)
    back = exchanged(du_rows.reshape(n_rank, -1, width), ED).reshape(-1, width)
    du = dot(both, back, ((1,), (0,))) + through_router
    gain_part = jnp.sum(du * h_wide * inv, axis=0, keepdims=True)
    w = du * gain
    proj = jnp.mean(w * h_wide, axis=-1, keepdims=True)
    out = (g_wide + inv * w - h_wide * (inv * inv * inv) * proj).astype(jnp.bfloat16)
    return out, (dy, q, router_part, gain_part)


def local(x_in, cotangent, route_ids, norm_gain, router, w_gate_up, w_down):
    micro_count, tok_rows, cols = x_in.shape
    n_section = lax.axis_size("section")
    n_rank = lax.axis_size("expert") * lax.axis_size("dp")
    n_expert = router.shape[2]
    width = w_down.shape[3]
    half_micro = micro_count // 2
    stages = n_section // 2
    capacity = tok_rows * 2 // n_expert
    section = lax.axis_index("section")
    lane = section % 2
    stage = section // 2
    first = lane == 0

    x_lo, x_hi = x_in[:half_micro], x_in[half_micro:]
    c_lo, c_hi = cotangent[:half_micro], cotangent[half_micro:]
    sent = jnp.stack([x_lo, x_hi] * (n_section // 4) + [c_lo, c_hi] * (n_section // 4))
    landed = exchanged(sent, "section")
    seed = jnp.transpose(landed, (1, 2, 0, 3)).reshape(half_micro * tok_rows, width)

    own_gu, own_dn = w_gate_up[0, 0], w_down[0, 0]
    gu_a, gu_b = chosen(first, own_gu, swapped(own_gu))
    dn_a, dn_b = chosen(first, own_dn, swapped(own_dn))
    rt_a, rt_b = chosen(first, router[0], swapped(router[0]))
    gn_a, gn_b = chosen(first, norm_gain, swapped(norm_gain))
    id_a, id_b = chosen(first, route_ids[0], swapped(route_ids[0]))
    id_a, id_b = (lax.dynamic_slice_in_dim(r, lane * half_micro, half_micro, 0) for r in (id_a, id_b))
    wt_a = (*route_tables(id_a, n_expert, capacity), gn_a, rt_a, gu_a, dn_a)
    wt_b = (*route_tables(id_b, n_expert, capacity), gn_b, rt_b, gu_b, dn_b)

    h_in = seed
    for step in range(stages):
        h_mid, saved_a = forward_layer(h_in, wt_a, n_rank)
        if step + 1 < stages:
            h_out, saved_b = forward_layer(h_mid, wt_b, n_rank)
            h_in = jnp.where(stage == step + 1, rotated(h_out, 2), h_in)
        else:
            _, saved_b = forward_layer(h_mid, wt_b, n_rank)

    grad = seed
    for step in range(stages):
        mid, parts_b = backward_layer(grad, wt_b, saved_b, n_rank)
        low, parts_a = backward_layer(mid, wt_a, saved_a, n_rank)
        if step + 1 < stages:
            grad = jnp.where(stage == stages - 2 - step, rotated(low, -2), grad)

    pieces = jnp.transpose(low.reshape(half_micro, tok_rows, n_section, cols), (2, 0, 1, 3))
    landed = exchanged(pieces, "section")
    grad_in = jnp.concatenate([landed[0], landed[1]], axis=0)

    rows_mine, rows_other = chosen(first, saved_a[5], saved_b[5])
    hid_mine, hid_other = chosen(first, saved_a[7], saved_b[7])
    dy_mine, dy_other = chosen(first, parts_a[0], parts_b[0])
    q_mine, q_other = chosen(first, parts_a[1], parts_b[1])
    all_rows = jnp.concatenate([rows_mine, swapped(rows_other)], axis=0)
    all_hid = jnp.concatenate([hid_mine, swapped(hid_other)], axis=0)
    all_dy = jnp.concatenate([dy_mine, swapped(dy_other)], axis=0)
    all_q = jnp.concatenate([q_mine, swapped(q_other)], axis=0)
    grad_gu = dot(all_rows, all_q, ((0,), (0,)))
    grad_dn = dot(all_hid, all_dy, ((0,), (0,)))

    small_a = jnp.concatenate([parts_a[2], parts_a[3]], axis=0)
    small_b = jnp.concatenate([parts_b[2], parts_b[3]], axis=0)
    small_mine, small_other = chosen(first, small_a, small_b)
    small = (small_mine + swapped(small_other)).astype(jnp.bfloat16)
    copies = jnp.broadcast_to(small, (n_rank, *small.shape))
    total = jnp.sum(exchanged(copies, ED).astype(jnp.float32), axis=0)
    grad_router = jnp.transpose(total[:n_expert])
    grad_gain = total[n_expert]
    return (grad_in, grad_gu[None, None], grad_dn[None, None], grad_router[None], grad_gain[None])


def solution(mesh):
    in_specs = (
        P(None, ED, "section"),
        P(None, ED, "section"),
        P("section", None, ED, None),
        P("section", None),
        P("section", None, None),
        P("section", ED, None, None),
        P("section", ED, None, None),
    )
    out_specs = (
        P(None, ED, "section"),
        P("section", ED, None, None),
        P("section", ED, None, None),
        P("section", None, None),
        P("section", None),
    )
    return jax.shard_map(local, mesh=mesh, in_specs=in_specs, out_specs=out_specs, check_vma=False)
```

time: 1310 us -> 679 us (0.52)
  starting transfers between devices: 358 us -> 89 us
  blocking collectives: 0 us -> 208 us
  waiting for transfers between devices: 387 us -> 220 us
  other arithmetic: 167 us -> 33.6 us
  local copies, waits for them, and re-layouts: 152 us -> 20.4 us
  matrix products: 217 us -> 93.6 us
    all_to_all x0 -> x15, blocking collectives: none -> 208 us  [exchanged(): return lax.all_to_all(rows, axis, split_axis=0, concat_axis=0, tiled=True)]
    all_to_all x63 -> x20, starting transfers between devices: 286 us -> 82.8 us  [exchanged(): return lax.all_to_all(rows, axis, split_axis=0, concat_axis=0, tiled=True)]
    all_to_all x63 -> x20, waiting for transfers between devices: 311 us -> 180 us  [exchanged(): return lax.all_to_all(rows, axis, split_axis=0, concat_axis=0, tiled=True)]
    dot_general x212 -> x84, matrix products: 217 us -> 93.6 us  [dot(): lax.dot_general(a, b, (dims, ((), ())), preferred_element_type=jnp.float32)]
    dynamic_update_slice x105 -> x0, other arithmetic: 104 us -> none  [keep_row(): lax.dynamic_update_index_in_dim(stash, jnp.where(active, value, old_row),...]
    dynamic_slice x90 -> x0, local copies, waits for them, and re-layouts: 69.4 us -> none  [the longest x75 54.5 us: keep_row(): old_row = lax.dynamic_index_in_dim(stash, position, 0, keepdims=False)]
    ppermute x30 -> x16, starting transfers between devices: 71.8 us -> 6.26 us  [the longest x6 3.89 us: rotated(): lax.ppermute(value, 'section', [(s, (s + steps) % count) for s in range(c...]
    all_gather x1 -> x0, waiting for transfers between devices: 27 us -> none  [sent_together(): whole = lax.all_gather(both, axis, axis=dim, tiled=True)]
  transfers between devices with their start and end apart: 94 -> 36, of which waited for: 79 -> 27; matrix products, arithmetic and copies ran while one was open for 17% -> 9% of each run, Pallas kernels for 0% -> 0%
where the time goes in v1:
time: 679 us; the launch traced here: 668 us
  waiting for transfers between devices  220 us (32%)
  blocking collectives  208 us (31%)
  matrix products  93.6 us (14%)
  starting transfers between devices  89 us (13%)
  other arithmetic  33.6 us (5%)
  local copies, waits for them, and re-layouts  20.4 us (3%)
    all_to_all x15, blocking collectives, exchanged(): return lax.all_to_all(rows, axis, split_axis=0, concat_axis=0, tiled=True)  208 us
    all_to_all x20, waiting for transfers between devices, exchanged(): return lax.all_to_all(rows, axis, split_axis=0, concat_axis=0, tiled=True)  180 us
    dot_general x84, matrix products, dot(): lax.dot_general(a, b, (dims, ((), ())), preferred_element_type=jnp.float32)  93.6 us
    all_to_all x20, starting transfers between devices, exchanged(): return lax.all_to_all(rows, axis, split_axis=0, concat_axis=0, tiled=True)  82.8 us
    ppermute x6, waiting for transfers between devices, rotated(): lax.ppermute(value, 'section', [(s, (s + steps) % count) for s in range(c...  38.6 us
    unnamed x230, local copies, waits for them, and re-layouts  14 us
  transfers between devices with their start and end apart: 36, of which 27 were waited for; matrix products, arithmetic and copies ran while one was open for 9% of the time, Pallas kernels for 0%

profile of v1, /device:TPU:0, one launch (start us, length us, event | category | flops | bytes accessed | tf_op | source)
XLA Modules:
  0.0 667.8 jit_solution(12432550314569827037)
XLA Ops:
  56.9 10.2 %all-to-all-done.2 = bf16[16,8,2048]{2,1,0:T(8,128)(2,1)S(1)} async-done(((bf16[16,8,2048]{2,1,0:T(8,128)(2,1)}), bf16[16,8,2048]{2,1,0:T(8,128)(2,1)S(1)}, u32[]{:S(2)}, u32[]{:S(2)}) %all-to-all-start.2) | async-done | bytes 524320 | tf_op jit(solution)/shard_map/all_to_all | solution.py:21
  68.1 13.5 %all_to_all.175 = bf16[16,8,2048]{2,1,0:T(8,128)(2,1)S(1)} all-to-all(bf16[16,8,2048]{2,1,0:T(8,128)(2,1)S(1)} %fusion.2), channel_id=1, replica_groups=mesh['section'=8,'expert'=4,'dp'=4] {'expert','dp'}, dimensions={0} | all-to-all | bytes 1048576 | tf_op jit(solution)/shard_map/all_to_all | solution.py:21
  106.1 13.3 %all_to_all.176 = bf16[16,8,2048]{2,1,0:T(8,128)(2,1)S(1)} all-to-all(bf16[16,8,2048]{2,1,0:T(8,128)(2,1)S(1)} %fusion.4), channel_id=1, replica_groups=mesh['section'=8,'expert'=4,'dp'=4] {'expert','dp'}, dimensions={0} | all-to-all | bytes 1048576 | tf_op jit(solution)/shard_map/all_to_all | solution.py:21
  140.6 13.8 %all_to_all.177 = bf16[16,8,2048]{2,1,0:T(8,128)(2,1)S(1)} all-to-all(bf16[16,8,2048]{2,1,0:T(8,128)(2,1)S(1)} %fusion.6), channel_id=1, replica_groups=mesh['section'=8,'expert'=4,'dp'=4] {'expert','dp'}, dimensions={0} | all-to-all | bytes 1048576 | tf_op jit(solution)/shard_map/all_to_all | solution.py:21
  181.0 13.4 %all_to_all.178 = bf16[16,8,2048]{2,1,0:T(8,128)(2,1)S(1)} all-to-all(bf16[16,8,2048]{2,1,0:T(8,128)(2,1)S(1)} %fusion.8), channel_id=1, replica_groups=mesh['section'=8,'expert'=4,'dp'=4] {'expert','dp'}, dimensions={0} | all-to-all | bytes 1048576 | tf_op jit(solution)/shard_map/all_to_all | solution.py:21
  203.2 10.8 %all-to-all-done.10 = bf16[16,8,2048]{2,1,0:T(8,128)(2,1)S(1)} async-done(((bf16[16,8,2048]{2,1,0:T(8,128)(2,1)}), bf16[16,8,2048]{2,1,0:T(8,128)(2,1)S(1)}, u32[]{:S(2)}, u32[]{:S(2)}) %all-to-all-start.10) | async-done | bytes 524320 | tf_op jit(solution)/shard_map/all_to_all | solution.py:21
  217.1 15.5 %all_to_all.179 = bf16[16,8,2048]{2,1,0:T(8,128)(2,1)S(1)} all-to-all(bf16[16,8,2048]{2,1,0:T(8,128)(2,1)S(1)} %fusion.10), channel_id=1, replica_groups=mesh['section'=8,'expert'=4,'dp'=4] {'expert','dp'}, dimensions={0} | all-to-all | bytes 1048576 | tf_op jit(solution)/shard_map/all_to_all | solution.py:21
  259.6 14.2 %all_to_all.180 = bf16[16,8,2048]{2,1,0:T(8,128)(2,1)S(1)} all-to-all(bf16[16,8,2048]{2,1,0:T(8,128)(2,1)S(1)} %fusion.12), channel_id=1, replica_groups=mesh['section'=8,'expert'=4,'dp'=4] {'expert','dp'}, dimensions={0} | all-to-all | bytes 1048576 | tf_op jit(solution)/shard_map/all_to_all | solution.py:21
  296.9 13.4 %all_to_all.181 = bf16[16,8,2048]{2,1,0:T(8,128)(2,1)S(1)} all-to-all(bf16[16,8,2048]{2,1,0:T(8,128)(2,1)S(1)} %fusion.15), channel_id=1, replica_groups=mesh['section'=8,'expert'=4,'dp'=4] {'expert','dp'}, dimensions={0} | all-to-all | bytes 1048576 | tf_op jit(solution)/shard_map/all_to_all | solution.py:21
  331.3 13.6 %all_to_all.182 = bf16[16,8,2048]{2,1,0:T(8,128)(2,1)S(1)} all-to-all(bf16[16,8,2048]{2,1,0:T(8,128)(2,1)S(1)} %fusion.14), channel_id=1, replica_groups=mesh['section'=8,'expert'=4,'dp'=4] {'expert','dp'}, dimensions={0} | all-to-all | bytes 1048576 | tf_op jit(solution)/shard_map/all_to_all | solution.py:21
  347.4 13.3 %all_to_all.183 = bf16[16,8,2048]{2,1,0:T(8,128)(2,1)S(1)} all-to-all(bf16[16,8,2048]{2,1,0:T(8,128)(2,1)S(1)} %fusion.16), channel_id=1, replica_groups=mesh['section'=8,'expert'=4,'dp'=4] {'expert','dp'}, dimensions={0} | all-to-all | bytes 1048576 | tf_op jit(solution)/shard_map/all_to_all | solution.py:21
  362.5 13.6 %all_to_all.184 = bf16[16,8,2048]{2,1,0:T(8,128)(2,1)S(1)} all-to-all(bf16[16,8,2048]{2,1,0:T(8,128)(2,1)S(1)} %fusion.18), channel_id=1, replica_groups=mesh['section'=8,'expert'=4,'dp'=4] {'expert','dp'}, dimensions={0} | all-to-all | bytes 1048576 | tf_op jit(solution)/shard_map/all_to_all | solution.py:21
  383.7 10.1 %all-to-all-done.20 = bf16[16,8,2048]{2,1,0:T(8,128)(2,1)} async-done(((bf16[16,8,2048]{2,1,0:T(8,128)(2,1)}), bf16[16,8,2048]{2,1,0:T(8,128)(2,1)}, u32[]{:S(2)}, u32[]{:S(2)}) %all-to-all-start.20) | async-done | bytes 524320 | tf_op jit(solution)/shard_map/all_to_all | solution.py:21
  403.1 15.0 %all_to_all.185 = bf16[16,8,2048]{2,1,0:T(8,128)(2,1)S(1)} all-to-all(bf16[16,8,2048]{2,1,0:T(8,128)(2,1)S(1)} %fusion.20), channel_id=1, replica_groups=mesh['section'=8,'expert'=4,'dp'=4] {'expert','dp'}, dimensions={0} | all-to-all | bytes 1048576 | tf_op jit(solution)/shard_map/all_to_all | solution.py:21
  425.6 12.7 %all-to-all-done.22 = bf16[16,8,2048]{2,1,0:T(8,128)(2,1)} async-done(((bf16[16,8,2048]{2,1,0:T(8,128)(2,1)}), bf16[16,8,2048]{2,1,0:T(8,128)(2,1)}, u32[]{:S(2)}, u32[]{:S(2)}) %all-to-all-start.22) | async-done | bytes 524320 | tf_op jit(solution)/shard_map/all_to_all | solution.py:21
  441.0 13.9 %all_to_all.186 = bf16[16,8,2048]{2,1,0:T(8,128)(2,1)S(1)} all-to-all(bf16[16,8,2048]{2,1,0:T(8,128)(2,1)S(1)} %fusion.22), channel_id=1, replica_groups=mesh['section'=8,'expert'=4,'dp'=4] {'expert','dp'}, dimensions={0} | all-to-all | bytes 1048576 | tf_op jit(solution)/shard_map/all_to_all | solution.py:21
  462.3 10.4 %all-to-all-done.24 = bf16[16,8,2048]{2,1,0:T(8,128)(2,1)} async-done(((bf16[16,8,2048]{2,1,0:T(8,128)(2,1)}), bf16[16,8,2048]{2,1,0:T(8,128)(2,1)}, u32[]{:S(2)}, u32[]{:S(2)}) %all-to-all-start.24) | async-done | bytes 524320 | tf_op jit(solution)/shard_map/all_to_all | solution.py:21
  481.9 13.8 %all_to_all.187 = bf16[16,8,2048]{2,1,0:T(8,128)(2,1)S(1)} all-to-all(bf16[16,8,2048]{2,1,0:T(8,128)(2,1)S(1)} %fusion.24), channel_id=1, replica_groups=mesh['section'=8,'expert'=4,'dp'=4] {'expert','dp'}, dimensions={0} | all-to-all | bytes 1048576 | tf_op jit(solution)/shard_map/all_to_all | solution.py:21
  502.5 10.0 %all-to-all-done.26 = bf16[16,8,2048]{2,1,0:T(8,128)(2,1)S(1)} async-done(((bf16[16,8,2048]{2,1,0:T(8,128)(2,1)}), bf16[16,8,2048]{2,1,0:T(8,128)(2,1)S(1)}, u32[]{:S(2)}, u32[]{:S(2)}) %all-to-all-start.26) | async-done | bytes 524320 | tf_op jit(solution)/shard_map/all_to_all | solution.py:21
  514.2 13.9 %all_to_all.188 = bf16[16,8,2048]{2,1,0:T(8,128)(2,1)S(1)} all-to-all(bf16[16,8,2048]{2,1,0:T(8,128)(2,1)S(1)} %fusion.26), channel_id=1, replica_groups=mesh['section'=8,'expert'=4,'dp'=4] {'expert','dp'}, dimensions={0} | all-to-all | bytes 1048576 | tf_op jit(solution)/shard_map/all_to_all | solution.py:21
  534.9 10.0 %all-to-all-done.28 = bf16[16,8,2048]{2,1,0:T(8,128)(2,1)S(1)} async-done(((bf16[16,8,2048]{2,1,0:T(8,128)(2,1)}), bf16[16,8,2048]{2,1,0:T(8,128)(2,1)S(1)}, u32[]{:S(2)}, u32[]{:S(2)}) %all-to-all-start.28) | async-done | bytes 524320 | tf_op jit(solution)/shard_map/all_to_all | solution.py:21
  554.2 13.8 %all_to_all.189 = bf16[16,8,2048]{2,1,0:T(8,128)(2,1)S(1)} all-to-all(bf16[16,8,2048]{2,1,0:T(8,128)(2,1)S(1)} %fusion.28), channel_id=1, replica_groups=mesh['section'=8,'expert'=4,'dp'=4] {'expert','dp'}, dimensions={0} | all-to-all | bytes 1048576 | tf_op jit(solution)/shard_map/all_to_all | solution.py:21
  574.9 10.0 %all-to-all-done.30 = bf16[16,8,2048]{2,1,0:T(8,128)(2,1)S(1)} async-done(((bf16[16,8,2048]{2,1,0:T(8,128)(2,1)}), bf16[16,8,2048]{2,1,0:T(8,128)(2,1)S(1)}, u32[]{:S(2)}, u32[]{:S(2)}) %all-to-all-start.30) | async-done | bytes 524320 | tf_op jit(solution)/shard_map/all_to_all | solution.py:21
  655.1 10.1 %all-to-all-done.34 = bf16[16,17,2048]{2,1,0:T(8,128)(2,1)S(1)} async-done(((bf16[16,17,2048]{2,1,0:T(8,128)(2,1)}), bf16[16,17,2048]{2,1,0:T(8,128)(2,1)S(1)}, u32[]{:S(2)}, u32[]{:S(2)}) %all-to-all-start.34) | async-done | bytes 1114144 | tf_op jit(solution)/shard_map/all_to_all | solution.py:21
  (485 shorter events, 362.2 us)
Async XLA Ops:
  1.3 16.9 %collective-permute-start = (s32[8,16,2]{1,0,2:T(8,128)S(1)}, s32[8,16,2]{1,0,2:T(8,128)S(1)}, u32[]{:S(2)}, u32[]{:S(2)}) collective-permute-start(s32[8,16,2]{1,0,2:T(8,128)S(1)} %bitcast.358), channel_id=1, source_target_pairs={{0,16},{16,0},{32,48},{48,32},{64,80},{80,64},{96,112},{112,96},{1... | collective-permute-start | bytes 3080 | tf_op jit(solution)/shard_map/ppermute | solution.py:12
  1.4 19.2 %collective-permute-start.1 = (f32[1,2048]{1,0:T(1,128)}, f32[1,2048]{1,0:T(1,128)S(1)}, u32[]{:S(2)}, u32[]{:S(2)}) collective-permute-start(f32[1,2048]{1,0:T(1,128)} %param.10), channel_id=1, source_target_pairs={{0,16},{16,0},{32,48},{48,32},{64,80},{80,64},{96,112},{112,96},{1... | collective-permute-start | bytes 24584 | tf_op jit(solution)/shard_map/ppermute | solution.py:12
  1.9 54.7 %collective-permute-start.2 = (bf16[2048,16]{0,1:T(8,128)(2,1)}, bf16[2048,16]{0,1:T(8,128)(2,1)S(1)}, u32[]{:S(2)}, u32[]{:S(2)}) collective-permute-start(bf16[2048,16]{0,1:T(8,128)(2,1)} %bitcast.357), channel_id=1, source_target_pairs={{0,16},{16,0},{32,48},{48,32},{64,80},{80,64},{96,112},{112,96},{1... | collective-permute-start | bytes 196616 | tf_op jit(solution)/shard_map/ppermute | solution.py:12
  1.9 37.1 %collective-permute-start.3 = (bf16[2048,1024]{1,0:T(8,128)(2,1)}, bf16[2048,1024]{1,0:T(8,128)(2,1)}, u32[]{:S(2)}, u32[]{:S(2)}) collective-permute-start(bf16[2048,1024]{1,0:T(8,128)(2,1)} %bitcast.319), channel_id=1, source_target_pairs={{0,16},{16,0},{32,48},{48,32},{64,80},{80,64},{96,112},{112,96},{1... | collective-permute-start | bytes 12582920 | tf_op jit(solution)/shard_map/ppermute | solution.py:12
  17.8 17.2 %collective-permute-start.4 = (bf16[512,2048]{1,0:T(8,128)(2,1)}, bf16[512,2048]{1,0:T(8,128)(2,1)}, u32[]{:S(2)}, u32[]{:S(2)}) collective-permute-start(bf16[512,2048]{1,0:T(8,128)(2,1)} %bitcast.321), channel_id=1, source_target_pairs={{0,16},{16,0},{32,48},{48,32},{64,80},{80,64},{96,112},{112,96},{1... | collective-permute-start | bytes 6291464 | tf_op jit(solution)/shard_map/ppermute | solution.py:12
  26.9 19.2 %all-to-all-start.1 = ((bf16[16,8,2048]{2,1,0:T(8,128)(2,1)}), bf16[16,8,2048]{2,1,0:T(8,128)(2,1)S(1)}, u32[]{:S(2)}, u32[]{:S(2)}) async-start(bf16[16,8,2048]{2,1,0:T(8,128)(2,1)} %fusion), calls=%async_computation.1 | async-start | bytes 1048576 | tf_op jit(solution)/shard_map/all_to_all | solution.py:21
  50.5 16.7 %all-to-all-start.2 = ((bf16[16,8,2048]{2,1,0:T(8,128)(2,1)}), bf16[16,8,2048]{2,1,0:T(8,128)(2,1)S(1)}, u32[]{:S(2)}, u32[]{:S(2)}) async-start(bf16[16,8,2048]{2,1,0:T(8,128)(2,1)} %fusion.1), calls=%async_computation.2 | async-start | bytes 1048576 | tf_op jit(solution)/shard_map/all_to_all | solution.py:21
  83.7 13.6 %all-to-all-start.4 = ((bf16[16,8,2048]{2,1,0:T(8,128)(2,1)}), bf16[16,8,2048]{2,1,0:T(8,128)(2,1)S(1)}, u32[]{:S(2)}, u32[]{:S(2)}) async-start(bf16[16,8,2048]{2,1,0:T(8,128)(2,1)} %fusion.3), calls=%async_computation.4 | async-start | bytes 1048576 | tf_op jit(solution)/shard_map/all_to_all | solution.py:21
  123.9 13.6 %all-to-all-start.6 = ((bf16[16,8,2048]{2,1,0:T(8,128)(2,1)}), bf16[16,8,2048]{2,1,0:T(8,128)(2,1)S(1)}, u32[]{:S(2)}, u32[]{:S(2)}) async-start(bf16[16,8,2048]{2,1,0:T(8,128)(2,1)} %fusion.5), calls=%async_computation.6 | async-start | bytes 1048576 | tf_op jit(solution)/shard_map/all_to_all | solution.py:21
  156.5 13.6 %all-to-all-start.8 = ((bf16[16,8,2048]{2,1,0:T(8,128)(2,1)}), bf16[16,8,2048]{2,1,0:T(8,128)(2,1)S(1)}, u32[]{:S(2)}, u32[]{:S(2)}) async-start(bf16[16,8,2048]{2,1,0:T(8,128)(2,1)} %fusion.7), calls=%async_computation.8 | async-start | bytes 1048576 | tf_op jit(solution)/shard_map/all_to_all | solution.py:21
  198.8 15.2 %all-to-all-start.10 = ((bf16[16,8,2048]{2,1,0:T(8,128)(2,1)}), bf16[16,8,2048]{2,1,0:T(8,128)(2,1)S(1)}, u32[]{:S(2)}, u32[]{:S(2)}) async-start(bf16[16,8,2048]{2,1,0:T(8,128)(2,1)} %fusion.9), calls=%async_computation.10 | async-start | bytes 1048576 | tf_op jit(solution)/shard_map/all_to_all | solution.py:21
  234.7 13.7 %all-to-all-start.12 = ((bf16[16,8,2048]{2,1,0:T(8,128)(2,1)}), bf16[16,8,2048]{2,1,0:T(8,128)(2,1)S(1)}, u32[]{:S(2)}, u32[]{:S(2)}) async-start(bf16[16,8,2048]{2,1,0:T(8,128)(2,1)} %fusion.11), calls=%async_computation.12 | async-start | bytes 1048576 | tf_op jit(solution)/shard_map/all_to_all | solution.py:21
  278.3 14.4 %all-to-all-start.14 = ((bf16[16,8,2048]{2,1,0:T(8,128)(2,1)}), bf16[16,8,2048]{2,1,0:T(8,128)(2,1)}, u32[]{:S(2)}, u32[]{:S(2)}) async-start(bf16[16,8,2048]{2,1,0:T(8,128)(2,1)} %fusion.13), calls=%async_computation.14 | async-start | bytes 1048576 | tf_op jit(solution)/shard_map/all_to_all | solution.py:21
  314.2 13.8 %all-to-all-start.18 = ((bf16[16,8,2048]{2,1,0:T(8,128)(2,1)}), bf16[16,8,2048]{2,1,0:T(8,128)(2,1)S(1)}, u32[]{:S(2)}, u32[]{:S(2)}) async-start(bf16[16,8,2048]{2,1,0:T(8,128)(2,1)} %fusion.17), calls=%async_computation.18 | async-start | bytes 1048576 | tf_op jit(solution)/shard_map/all_to_all | solution.py:21
  379.3 14.5 %all-to-all-start.20 = ((bf16[16,8,2048]{2,1,0:T(8,128)(2,1)}), bf16[16,8,2048]{2,1,0:T(8,128)(2,1)}, u32[]{:S(2)}, u32[]{:S(2)}) async-start(bf16[16,8,2048]{2,1,0:T(8,128)(2,1)} %fusion.19), calls=%async_computation.20 | async-start | bytes 1048576 | tf_op jit(solution)/shard_map/all_to_all | solution.py:21
  421.4 17.0 %all-to-all-start.22 = ((bf16[16,8,2048]{2,1,0:T(8,128)(2,1)}), bf16[16,8,2048]{2,1,0:T(8,128)(2,1)}, u32[]{:S(2)}, u32[]{:S(2)}) async-start(bf16[16,8,2048]{2,1,0:T(8,128)(2,1)} %fusion.21), calls=%async_computation.22 | async-start | bytes 1048576 | tf_op jit(solution)/shard_map/all_to_all | solution.py:21
  458.1 14.7 %all-to-all-start.24 = ((bf16[16,8,2048]{2,1,0:T(8,128)(2,1)}), bf16[16,8,2048]{2,1,0:T(8,128)(2,1)}, u32[]{:S(2)}, u32[]{:S(2)}) async-start(bf16[16,8,2048]{2,1,0:T(8,128)(2,1)} %fusion.23), calls=%async_computation.24 | async-start | bytes 1048576 | tf_op jit(solution)/shard_map/all_to_all | solution.py:21
  498.9 13.6 %all-to-all-start.26 = ((bf16[16,8,2048]{2,1,0:T(8,128)(2,1)}), bf16[16,8,2048]{2,1,0:T(8,128)(2,1)S(1)}, u32[]{:S(2)}, u32[]{:S(2)}) async-start(bf16[16,8,2048]{2,1,0:T(8,128)(2,1)} %fusion.25), calls=%async_computation.26 | async-start | bytes 1048576 | tf_op jit(solution)/shard_map/all_to_all | solution.py:21
  531.3 13.6 %all-to-all-start.28 = ((bf16[16,8,2048]{2,1,0:T(8,128)(2,1)}), bf16[16,8,2048]{2,1,0:T(8,128)(2,1)S(1)}, u32[]{:S(2)}, u32[]{:S(2)}) async-start(bf16[16,8,2048]{2,1,0:T(8,128)(2,1)} %fusion.27), calls=%async_computation.28 | async-start | bytes 1048576 | tf_op jit(solution)/shard_map/all_to_all | solution.py:21
  571.3 13.6 %all-to-all-start.30 = ((bf16[16,8,2048]{2,1,0:T(8,128)(2,1)}), bf16[16,8,2048]{2,1,0:T(8,128)(2,1)S(1)}, u32[]{:S(2)}, u32[]{:S(2)}) async-start(bf16[16,8,2048]{2,1,0:T(8,128)(2,1)} %fusion.29), calls=%async_computation.30 | async-start | bytes 1048576 | tf_op jit(solution)/shard_map/all_to_all | solution.py:21
  588.4 13.6 %all-to-all-start.31 = ((bf16[16,8,2048]{2,1,0:T(8,128)(2,1)}), bf16[16,8,2048]{2,1,0:T(8,128)(2,1)S(1)}, u32[]{:S(2)}, u32[]{:S(2)}) async-start(bf16[16,8,2048]{2,1,0:T(8,128)(2,1)} %fusion.30), calls=%async_computation.31 | async-start | bytes 1048576 | tf_op jit(solution)/shard_map/all_to_all | solution.py:21
  592.9 50.9 %collective-permute-start.11 = (bf16[128,2048]{1,0:T(8,128)(2,1)}, bf16[128,2048]{1,0:T(8,128)(2,1)}, u32[]{:S(2)}, u32[]{:S(2)}) collective-permute-start(bf16[128,2048]{1,0:T(8,128)(2,1)} %get-tuple-element.61), channel_id=1, source_target_pairs={{0,16},{16,0},{32,48},{48,32},{64,80},{80,64},{96,112},{112,96},{1... | collective-permute-start | bytes 1572872 | tf_op jit(solution)/shard_map/ppermute | solution.py:12
  609.4 13.8 %all-to-all-start.32 = ((bf16[16,8,2048]{2,1,0:T(8,128)(2,1)}), bf16[16,8,2048]{2,1,0:T(8,128)(2,1)S(1)}, u32[]{:S(2)}, u32[]{:S(2)}) async-start(bf16[16,8,2048]{2,1,0:T(8,128)(2,1)} %fusion.31), calls=%async_computation.32 | async-start | bytes 1048576 | tf_op jit(solution)/shard_map/all_to_all | solution.py:21
  637.7 27.5 %all-to-all-start.34 = ((bf16[16,17,2048]{2,1,0:T(8,128)(2,1)}), bf16[16,17,2048]{2,1,0:T(8,128)(2,1)S(1)}, u32[]{:S(2)}, u32[]{:S(2)}) async-start(bf16[16,17,2048]{2,1,0:T(8,128)(2,1)} %broadcast_in_dim.16), calls=%async_computation.34 | async-start | bytes 3145728 | tf_op jit(solution)/shard_map/all_to_all | solution.py:21
  (122 other events, 1700.9 us)
